TPU v7x, 32 devices: a whole 2x2x4 slice. The times are simulated.
32 devices in a mesh: groups: 2 (over y), expert: 4 (over x, core), tensor: 4 (over z).
Axes of the slice: x: 2, y: 2, z: 4, core: 2. Of those that a mesh axis runs over, the one named last changes fastest.
Arguments:
- tokens: bfloat16 [512, 4096], P(('groups', 'expert'), 'tensor'), parts along dimension 0, may hold values from -400 to 400
- norm_gain: float32 [4096], replicated, may hold values from 0.5 to 1.5
- w_gate: bfloat16 [4096, 65536], P(None, ('expert', 'tensor')), may hold values from -0.09375 to 0.09375
- w_up: bfloat16 [4096, 65536], P(None, ('expert', 'tensor')), may hold values from -0.09375 to 0.09375
- w_down: bfloat16 [65536, 4096], P(('expert', 'tensor')), may hold values from -0.0625 to 0.0625
- expert_ids: int32 [512, 2], P(('groups', 'expert')), parts along dimension 0, may hold values from 0 to 7, all different within a row; in each aligned block of 64 rows (0 to 63, 64 to 127, ...) at most 32 rows name the same one
- gate_weights: float32 [512, 2], P(('groups', 'expert')), parts along dimension 0, may hold values from 0.1 to 1
Outputs:
- moe_out: bfloat16 [512, 4096], P(('groups', 'expert'), 'tensor'), parts along dimension 0
There are 2 independent parts, one for each index of `groups`. A program takes and returns all parts, laid end to end along the dimension named above; an argument that names none is the same for every part. Nothing has to cross between parts.
Inputs may be any that keep to these rules, and one draw needn't show every extreme that they name: `expert_ids`: each request names two different experts. Within the rows of one device (aligned blocks of 64 rows) no expert is named by more than 32 rows, and in some blocks one expert is named by exactly 32 rows.
All inputs are finite; a program needn't handle non-finite values.
Results may differ from a plain program's by a relative error of at most 0.008.
Values may be sent and summed in bfloat16 or wider, within the bound.
A program may use at most 192 MiB of HBM per device.

v0:
```python
import jax
import jax.numpy as jnp
from jax import lax
from jax.sharding import PartitionSpec as P

EXPERTS = 8


def lookup(targets, token_table, valid_table):
    select = (targets[..., None] == jnp.arange(token_table.shape[0], dtype=jnp.int32)).astype(
        jnp.int32
    )
    token_at = jnp.sum(select[..., None] * token_table, axis=-2)
    valid_at = jnp.sum(select[..., None] * valid_table, axis=-2)
    return (token_at, valid_at)


def pack_rows(normed, targets, token_table, valid_table):
    token_at, valid_at = lookup(targets, token_table, valid_table)
    picked = jnp.take(normed, token_at.reshape(-1), axis=0)
    picked = picked.reshape(token_at.shape + (normed.shape[1],))
    return picked * valid_at[..., None].astype(jnp.bfloat16)


def per_device(tokens, norm_gain, w_gate, w_up, w_down, expert_ids, gate_weights):
    n_expert = lax.axis_size("expert")
    n_tensor = lax.axis_size("tensor")
    tok_rows = tokens.shape[0]
    width_local = tokens.shape[1]
    width_full = width_local * n_tensor
    capacity = tok_rows // 2
    per_expert = n_expert * n_tensor // EXPERTS
    tensor_index = lax.axis_index("tensor")
    peers = jnp.arange(n_expert, dtype=jnp.int32)
    own_targets = ((peers * n_tensor + tensor_index) // per_expert)[:, None]
    flat_ids = expert_ids.reshape(-1)
    onehot = (flat_ids[:, None] == jnp.arange(EXPERTS, dtype=jnp.int32)[None, :]).astype(jnp.int32)
    running = jnp.cumsum(onehot, axis=0)
    slot_of = jnp.sum(running * onehot, axis=1) - 1
    pair_token = jnp.arange(flat_ids.shape[0], dtype=jnp.int32) // 2
    slot_hits = onehot[:, :, None] * (
        slot_of[:, None, None] == jnp.arange(capacity, dtype=jnp.int32)[None, None, :]
    ).astype(jnp.int32)
    token_table = jnp.sum(slot_hits * pair_token[:, None, None], axis=0)
    valid_table = jnp.sum(slot_hits, axis=0)
    full_rows = lax.all_gather(tokens, "tensor", axis=1, tiled=True)
    values = full_rows.astype(jnp.float32)
    sum_squares = jnp.sum(values * values, axis=1)
    scale = lax.rsqrt(sum_squares / width_full + 1e-05)
    normed = (values * scale[:, None] * norm_gain[None, :]).astype(jnp.bfloat16)
    outbound = pack_rows(normed, own_targets, token_table, valid_table)
    own_block = lax.all_to_all(outbound, "expert", split_axis=0, concat_axis=0, tiled=True)
    items = own_block.shape[2]
    flattened = own_block.reshape(-1, own_block.shape[3])
    gate_act = jnp.dot(flattened, w_gate, preferred_element_type=jnp.float32)
    up_act = jnp.dot(flattened, w_up, preferred_element_type=jnp.float32)
    hidden = (jax.nn.silu(gate_act) * up_act).astype(jnp.bfloat16)
    partial_value = jnp.dot(hidden, w_down, preferred_element_type=jnp.float32)
    partial_value = partial_value.reshape(n_expert, 1, items, partial_value.shape[1])
    returned = lax.all_to_all(partial_value, "expert", split_axis=0, concat_axis=0, tiled=True)
    mixing = (
        jnp.arange(EXPERTS, dtype=jnp.int32)[:, None] == own_targets.reshape(-1)[None, :]
    ).astype(jnp.float32)
    out_width = returned.shape[3]
    by_expert = jnp.dot(
        mixing,
        returned.reshape(own_targets.size, -1),
        precision=lax.Precision.HIGHEST,
        preferred_element_type=jnp.float32,
    )
    by_expert = by_expert.reshape(EXPERTS * capacity, out_width)
    picks = jnp.take(by_expert, flat_ids * capacity + slot_of, axis=0)
    mixed = jnp.sum(picks.reshape(tok_rows, 2, out_width) * gate_weights[:, :, None], axis=1)
    mixed = lax.psum_scatter(mixed, "tensor", scatter_dimension=1, tiled=True)
    return mixed.astype(jnp.bfloat16)


def solution(mesh):
    in_specs = (
        P(("groups", "expert"), "tensor"),
        P(),
        P(None, ("expert", "tensor")),
        P(None, ("expert", "tensor")),
        P(("expert", "tensor"), None),
        P(("groups", "expert"), None),
        P(("groups", "expert"), None),
    )
    out_specs = P(("groups", "expert"), "tensor")
    return jax.shard_map(
        per_device, mesh=mesh, in_specs=in_specs, out_specs=out_specs, check_vma=False
    )
```

profile of v0, /device:TPU:0, one launch (start us, length us, event | category | flops | bytes accessed | tf_op | source)
XLA Modules:
  0.0 173.0 jit_solution(17244527256869342859)
XLA Ops:
  6.5 0.8 copy.25
  7.6 0.2 reduce_window_sum.11
  7.8 0.2 select_reduce_fusion
  8.1 0.3 multiply_reduce_fusion.1
  8.6 17.6 %all_gather.3 = bf16[64,4096]{1,0:T(8,128)(2,1)S(1)} all-gather(bf16[64,1024]{1,0:T(8,128)(2,1)} %param.7), channel_id=1, replica_groups=mesh['groups'=2,'expert'=4,'tensor'=4] {'tensor'}, dimensions={1}, use_global_device_ids=true | all-gather | bytes 655360 | tf_op jit(solution)/shard_map/all_gather | solution.py:46
  26.2 0.2 fusion.7
  26.4 0.9 fusion.9
  27.4 1.2 gather_fusion
  28.6 0.2 select_multiply_fusion
  28.8 17.0 %all_to_all.10 = bf16[4,1,32,4096]{3,2,1,0:T(8,128)(2,1)S(1)} all-to-all(bf16[4,1,32,4096]{3,2,1,0:T(8,128)(2,1)S(1)} %select_multiply_fusion), channel_id=1, replica_groups=mesh['groups'=2,'expert'=4,'tensor'=4] {'expert'}, dimensions={0} | all-to-all | bytes 2097152 | tf_op jit(solution)/shard_map/all_to_all | solution.py:52
  45.7 12.9 %fusion.20 = f32[128,4096]{1,0:T(8,128)S(1)} fusion(bf16[128,4096]{1,0:T(8,128)(2,1)S(1)} %bitcast.26, bf16[4096,4096]{1,0:T(8,128)(2,1)} %param.9), kind=kOutput, calls=%fused_computation.56 | convolution fusion | flops 4294967296 | bytes 36700160 | tf_op jit(solution)/shard_map/dot_general | solution.py:55
  58.7 25.3 %fusion.1 = f32[128,4096]{1,0:T(8,128)} fusion(bf16[4096,4096]{1,0:T(8,128)(2,1)} %param.11, bf16[128,4096]{1,0:T(8,128)(2,1)S(1)} %bitcast.27, bf16[4096,4096]{1,0:T(8,128)(2,1)} %param.10, f32[128,4096]{1,0:T(8,128)S(1)} %fusion.20), kind=kOutput, calls=%fused_computation.4 | convolution fusion | flops 8593080320 | bytes 72351744 | tf_op jit(solution)/shard_map/dot_general | solution.py:58
  84.0 3.7 %all-to-all-start.1 = ((f32[4,1,32,4096]{3,2,1,0:T(8,128)}), f32[4,1,32,4096]{3,2,1,0:T(8,128)S(1)}, u32[]{:S(2)}, u32[]{:S(2)}) async-start(f32[4,1,32,4096]{3,2,1,0:T(8,128)} %bitcast.29), calls=%async_computation.1 | async-start | bytes 4194304 | tf_op jit(solution)/shard_map/all_to_all | solution.py:60
  87.8 0.2 reduce-scatter.2.cloned.1.call-start
  88.2 0.1 mul.167
  88.7 24.7 %all-to-all-done.1 = f32[4,1,32,4096]{3,2,1,0:T(8,128)S(1)} async-done(((f32[4,1,32,4096]{3,2,1,0:T(8,128)}), f32[4,1,32,4096]{3,2,1,0:T(8,128)S(1)}, u32[]{:S(2)}, u32[]{:S(2)}) %all-to-all-start.1) | async-done | bytes 2097184 | tf_op jit(solution)/shard_map/all_to_all | solution.py:60
  113.4 1.4 copy.33
  114.7 4.0 %fusion.14 = f32[8,131072]{1,0:T(8,128)} fusion(f32[4,131072]{1,0:T(4,128)S(1)} %bitcast.24, s32[4]{0:T(128)S(1)} %and_select_fusion.1), kind=kOutput, calls=%fused_computation.32 | convolution fusion | flops 50331680 | bytes 6291472 | tf_op jit(solution)/shard_map/dot_general | solution.py:65
  118.8 4.9 %reshape.296 = f32[256,4096]{1,0:T(8,128)} reshape(f32[8,131072]{1,0:T(8,128)} %fusion.14) | data formatting | bytes 8388608 | tf_op jit(solution)/shard_map/reshape | solution.py:71
  123.6 5.6 %gather_fusion.1 = f32[128,4096]{1,0:T(8,128)} fusion(f32[256,4096]{1,0:T(8,128)} %reshape.296, s32[1024]{0:T(1024)S(1)} %pad_clamp_fusion), kind=kCustom, calls=%fused_computation.1 | custom fusion | bytes 4194816 | tf_op jit(solution)/shard_map/jit(_take)/gather | solution.py:72
  129.3 2.5 %gather.15 = f32[64,2,4096]{2,1,0:T(2,128)S(1)} reshape(f32[128,4096]{1,0:T(8,128)} %gather_fusion.1) | data formatting | bytes 4194304 | tf_op jit(solution)/shard_map/jit(_take)/gather | solution.py:72
  131.8 4.5 %multiply_reduce_fusion = f32[64,4096]{1,0:T(8,128)} fusion(f32[64,2,4096]{2,1,0:T(2,128)S(1)} %gather.15, pred[64,2]{1,0:T(8,128)(4,1)S(1)} %copy.27, f32[64,2]{1,0:T(8,128)S(1)} %copy.32), kind=kLoop, calls=%fused_computation.5 | loop fusion | flops 1310720 | bytes 3146368 | tf_op jit(solution)/shard_map/reduce_sum | solution.py:73
  136.3 28.3 %reduce-scatter.2.cloned.1.call-done = f32[64,1024]{1,0:T(8,128)} async-done(((f32[64,4096]{1,0:T(8,128)}), f32[64,1024]{1,0:T(8,128)}) %reduce-scatter.2.cloned.1.call-update) | async-done | bytes 262160 | tf_op jit(solution)/shard_map/reduce_scatter | solution.py:74
  164.6 1.6 convert_element_type.52
  (29 shorter events, 1.1 us)
Async XLA Ops:
  84.0 4.1 %copy-start = (s32[64,2]{0,1:T(2,128)S(1)}, s32[64,2]{0,1:T(2,128)}, u32[]{:S(2)}) copy-start(s32[64,2]{0,1:T(2,128)} %param.12) | copy-start | bytes 1540
  84.0 4.6 %copy-start.1 = (f32[64,2]{0,1:T(2,128)S(1)}, f32[64,2]{0,1:T(2,128)}, u32[]{:S(2)}) copy-start(f32[64,2]{0,1:T(2,128)} %param.13) | copy-start | bytes 1540
  84.0 29.4 %all-to-all-start.1 = ((f32[4,1,32,4096]{3,2,1,0:T(8,128)}), f32[4,1,32,4096]{3,2,1,0:T(8,128)S(1)}, u32[]{:S(2)}, u32[]{:S(2)}) async-start(f32[4,1,32,4096]{3,2,1,0:T(8,128)} %bitcast.29), calls=%async_computation.1 | async-start | bytes 4194304 | tf_op jit(solution)/shard_map/all_to_all | solution.py:60
  87.8 76.8 %reduce-scatter.2.cloned.1.call-start = ((), (), s32[]{:S(2)}) async-start(), calls=%async_computation.3 | async-start | bytes 1310720 | tf_op jit(solution)/shard_map/reduce_scatter | solution.py:74
Sparse Core Ops, SparseCore 0:
  136.4 28.1 reduce-scatter.1
where the time goes:
time: 173 us
  waiting for transfers between devices  53 us (31%)
  matrix products  42.3 us (24%)
  blocking collectives  34.6 us (20%)
  local copies, waits for them, and re-layouts  17.2 us (10%)
  between operations  13.6 us (8%)
  other arithmetic  8.46 us (5%)
  starting transfers between devices  3.96 us (2%)
    reduce_scatter x1, waiting for transfers between devices, per_device(): mixed = lax.psum_scatter(mixed, 'tensor', scatter_dimension=1, tiled=True)  28.3 us
    dot_general x1, matrix products, per_device(): partial_value = jnp.dot(hidden, w_down, preferred_element_type=jnp.float32)  25.3 us
    all_to_all x1, waiting for transfers between devices, per_device(): lax.all_to_all(partial_value, 'expert', split_axis=0, concat_axis=0, tile...  24.7 us
    all_gather x1, blocking collectives, per_device(): full_rows = lax.all_gather(tokens, 'tensor', axis=1, tiled=True)  17.6 us
    all_to_all x1, blocking collectives, per_device(): lax.all_to_all(outbound, 'expert', split_axis=0, concat_axis=0, tiled=True)  17 us
    dot_general x1, matrix products, per_device(): gate_act = jnp.dot(flattened, w_gate, preferred_element_type=jnp.float32)  12.9 us
    gather x2, local copies, waits for them, and re-layouts, per_device(): picks = jnp.take(by_expert, flat_ids * capacity + slot_of, axis=0)  8.11 us
    reshape x1, local copies, waits for them, and re-layouts, per_device(): by_expert = by_expert.reshape(EXPERTS * capacity, out_width)  4.86 us
  transfers between devices with their start and end apart: 2, of which 2 were waited for; matrix products, arithmetic and copies ran while one was open for 0% of the time, Pallas kernels for 0%

commit v1 on v0

v1 whole, which is shorter than its diff:
```python
import functools

import jax
import jax.numpy as jnp
from jax import lax
from jax.experimental import pallas as pl
from jax.experimental.pallas import tpu as pltpu
from jax.sharding import PartitionSpec as P

EXPERTS = 8
MIB = 1 << 20
MESH = pl.DeviceIdType.MESH


def log2(value):
    power = value.bit_length() - 1
    assert 1 << power == value
    return power


def kernel(
    n_e, n_t, cap, chunk, pair_slots, lag,
    tokens, gain, meta, ids, w_gate, w_up, w_down,
    out,
    wbuf, blocks, metas, packed, hidden, wslot, place, sendbuf, recvbuf, zsend, zrecv,
    wsem, lsem, rsem, zsem, xsem, dsem, msend, mrecv, osend, orecv, ysend, yrecv,
):
    g, e, t = lax.axis_index("groups"), lax.axis_index("expert"), lax.axis_index("tensor")
    n_x = n_e // 2
    xi, core = e // 2, e % 2
    sibling = xi * 2 + (1 - core)
    rows, width_local = tokens.shape
    width = w_gate.shape[0]
    hid = w_gate.shape[1]
    per_expert = n_e * n_t // EXPERTS
    mine = (e * n_t + t) // per_expert
    gate_pairs = hid // chunk
    per_slice = width_local // chunk
    down_chunks = n_t * per_slice
    pairs = gate_pairs + down_chunks // 2

    def slice_of(s):
        return lax.rem(t + 1 + s, n_t)

    def weight_copy(src, slot):
        return pltpu.make_async_copy(src, wbuf.at[slot, pl.ds(0, src.shape[0])], wsem.at[slot])

    def columns(start, size):
        return pl.ds(pl.multiple_of(start, size), size)

    def down_columns(d):
        return columns(slice_of(d // per_slice) * width_local + (d % per_slice) * chunk, chunk)

    def start_pair(p):
        slot = (p % pair_slots) * 2

        @pl.when(p < gate_pairs)
        def _():
            cols = columns(p * chunk, chunk)
            weight_copy(w_gate.at[:, cols], slot).start()
            weight_copy(w_up.at[:, cols], slot + 1).start()

        @pl.when(jnp.logical_and(p >= gate_pairs, p < pairs))
        def _():
            d = (p - gate_pairs) * 2
            weight_copy(w_down.at[:, down_columns(d)], slot).start()
            weight_copy(w_down.at[:, down_columns(d + 1)], slot + 1).start()

    def block_copy(ej, q, send_sem, to):
        return pltpu.make_async_remote_copy(
            src_ref=blocks.at[ej, q], dst_ref=blocks.at[ej, q],
            send_sem=send_sem, recv_sem=rsem.at[ej, q], device_id=to, device_id_type=MESH,
        )

    def z_copy(s):
        return block_copy(e, t, zsem.at[s], (g, e, lax.rem(t + s, n_t)))

    def x_copy(o, s):
        return block_copy(e, lax.rem(t + s, n_t), xsem.at[o, s], (g, lax.rem(xi + o, n_x) * 2 + core, t))

    def d_copy(o, s):
        ej = lax.rem(xi + o, n_x) * 2 + core
        return block_copy(ej, lax.rem(t + s, n_t), dsem.at[o, s], (g, sibling, t))

    def arrived(ej, s):
        block_copy(ej, lax.rem(t + s, n_t), zsem.at[0], (g, sibling, t)).wait_recv()

    def meta_copy(o):
        return pltpu.make_async_remote_copy(
            src_ref=meta, dst_ref=metas.at[e], send_sem=msend.at[o], recv_sem=mrecv.at[e],
            device_id=(g, lax.rem(e + o, n_e), t), device_id_type=MESH,
        )

    def meta_arrived(o):
        ej = lax.rem(e + o, n_e)
        pltpu.make_async_remote_copy(
            src_ref=meta, dst_ref=metas.at[ej], send_sem=msend.at[0], recv_sem=mrecv.at[ej],
            device_id=(g, ej, t), device_id_type=MESH,
        ).wait_recv()

    own = pltpu.make_async_copy(tokens, blocks.at[e, t], lsem.at[0])
    own.start()
    own_meta = pltpu.make_async_copy(meta, metas.at[e], lsem.at[1])
    own_meta.start()
    barrier = pltpu.get_barrier_semaphore()
    for o in range(1, n_e):
        pl.semaphore_signal(barrier, inc=1, device_id=(g, lax.rem(e + o, n_e), t), device_id_type=MESH)
    for o in range(1, n_t):
        pl.semaphore_signal(barrier, inc=1, device_id=(g, e, lax.rem(t + o, n_t)), device_id_type=MESH)
    for p in range(min(pair_slots, pairs)):
        start_pair(jnp.int32(p))
    own.wait()
    own_meta.wait()

    slots = n_e * cap
    column = lax.broadcasted_iota(jnp.int32, (rows, slots), 1)
    expert_at = ((column >> log2(cap)) * n_t + t) >> log2(per_expert)
    member = jnp.logical_or(ids[:, 0:1] == expert_at, ids[:, 1:2] == expert_at)
    before = lax.broadcasted_iota(jnp.int32, (rows, rows), 1) < lax.broadcasted_iota(jnp.int32, (rows, rows), 0)
    rank = jnp.dot(
        before.astype(jnp.float32).astype(jnp.bfloat16),
        member.astype(jnp.float32).astype(jnp.bfloat16),
        preferred_element_type=jnp.float32,
    )
    hit = jnp.logical_and(member, rank == (column & (cap - 1)).astype(jnp.float32))
    place[...] = hit.astype(jnp.float32).astype(jnp.bfloat16)

    pl.semaphore_wait(barrier, n_e - 1 + n_t - 1)

    for o in range(1, n_e):
        meta_copy(o).start()
    for s in range(1, n_t):
        z_copy(s).start()

    lanes = meta.shape[1]
    upper = (
        lax.broadcasted_iota(jnp.int32, (lanes, lanes), 0) < lax.broadcasted_iota(jnp.int32, (lanes, lanes), 1)
    ).astype(jnp.float32).astype(jnp.bfloat16)

    def pick(ej):
        id0, id1 = metas[ej, 0:1, :], metas[ej, 1:2, :]
        target = mine.astype(jnp.float32)
        named = jnp.where(id0 == target, 1.0, 0.0) + jnp.where(id1 == target, 1.0, 0.0)
        order = jnp.dot(
            jnp.broadcast_to(named, (8, lanes)).astype(jnp.bfloat16), upper, preferred_element_type=jnp.float32
        )[0:1, :]
        slot = lax.broadcasted_iota(jnp.int32, (cap, lanes), 0).astype(jnp.float32)
        return jnp.where(slot == order, 1.0, 0.0) * named

    def pack(s):
        q = lax.rem(t + s, n_t)

        def one(ej, _):
            @pl.when(ej % 2 != core)
            def _():
                arrived(ej, s)

            select = pick(ej)[:, :rows].astype(jnp.bfloat16)
            picked = jnp.dot(select, blocks[ej, q], preferred_element_type=jnp.float32)
            packed[columns(ej * cap, cap), columns(q * width_local, width_local)] = picked.astype(jnp.bfloat16)
            return 0

        lax.fori_loop(0, n_e, one, 0)

    def relay(s):
        for o in range(1, n_x):
            arrived(lax.rem(xi + o, n_x) * 2 + core, s)
            d_copy(o, s).start()

    def forward(s):
        for o in range(1, n_x):
            x_copy(o, s).start()
        d_copy(0, s).start()

    forward(0)
    for o in range(1, n_e):
        meta_arrived(o)

    def dispatch(s, _):
        arrived(e, s)
        forward(s)
        relay(s - 1)
        pack(s - 1)
        return 0

    lax.fori_loop(1, n_t, dispatch, 0)
    relay(n_t - 1)
    pack(n_t - 1)

    def normalize(ej, _):
        at = columns(ej * cap, cap)
        weight = jnp.where(metas[ej, 0:1, :] == mine.astype(jnp.float32), metas[ej, 2:3, :], metas[ej, 3:4, :])
        wslot[at, :] = jnp.broadcast_to(jnp.sum(pick(ej) * weight, axis=1, keepdims=True), (cap, lanes))
        values = packed[at, :].astype(jnp.float32)
        scale = lax.rsqrt(jnp.sum(values * values, axis=1, keepdims=True) / width + 1e-05)
        packed[at, :] = (values * scale * gain[...]).astype(jnp.bfloat16)
        return 0

    lax.fori_loop(0, n_e, normalize, 0)

    def expert_in(j, _):
        slot = (j % pair_slots) * 2
        cols = columns(j * chunk, chunk)
        weight_copy(w_gate.at[:, cols], slot).wait()
        gate = jnp.dot(packed[...], wbuf[slot], preferred_element_type=jnp.float32)
        weight_copy(w_up.at[:, cols], slot + 1).wait()
        up = jnp.dot(packed[...], wbuf[slot + 1], preferred_element_type=jnp.float32)
        hidden[:, cols] = (gate / (1.0 + jnp.exp(-gate)) * up).astype(jnp.bfloat16)
        start_pair(j + pair_slots)
        return 0

    lax.fori_loop(0, gate_pairs, expert_in, 0)

    def o_copy(o, d):
        ej = lax.rem(e + o, n_e)
        return pltpu.make_async_remote_copy(
            src_ref=sendbuf.at[d, columns(ej * cap, cap)], dst_ref=recvbuf.at[d, columns(e * cap, cap)],
            send_sem=osend.at[o, d], recv_sem=orecv.at[e, d], device_id=(g, ej, t), device_id_type=MESH,
        )

    def o_arrived(o, d):
        ej = lax.rem(e + o, n_e)
        pltpu.make_async_remote_copy(
            src_ref=sendbuf.at[d, columns(ej * cap, cap)], dst_ref=recvbuf.at[d, columns(ej * cap, cap)],
            send_sem=osend.at[0, 0], recv_sem=orecv.at[ej, d], device_id=(g, ej, t), device_id_type=MESH,
        ).wait_recv()

    def y_copy(d):
        k, c = d // per_slice, d % per_slice
        return pltpu.make_async_remote_copy(
            src_ref=zsend.at[d], dst_ref=zrecv.at[t, c],
            send_sem=ysend.at[d], recv_sem=yrecv.at[t, c],
            device_id=(g, e, slice_of(k)), device_id_type=MESH,
        )

    def y_arrived(s, c):
        tj = lax.rem(t + s, n_t)
        pltpu.make_async_remote_copy(
            src_ref=zsend.at[0], dst_ref=zrecv.at[tj, c],
            send_sem=ysend.at[0], recv_sem=yrecv.at[tj, c],
            device_id=(g, e, tj), device_id_type=MESH,
        ).wait_recv()
        return zrecv[tj, c].astype(jnp.float32)

    def combined(d):
        for o in range(1, n_e):
            o_arrived(o, d)
        return jnp.dot(place[...], recvbuf[d], preferred_element_type=jnp.float32)

    def combine_and_send(d):
        zsend[d] = combined(d).astype(jnp.bfloat16)
        y_copy(d).start()

    def expert_out(d, _):
        slot = ((gate_pairs + d // 2) % pair_slots) * 2 + d % 2
        weight_copy(w_down.at[:, down_columns(d)], slot).wait()
        value = jnp.dot(hidden[...], wbuf[slot, 0:hid, :], preferred_element_type=jnp.float32)
        sendbuf[d] = (value * wslot[:, 0:1]).astype(jnp.bfloat16)
        for o in range(1, n_e):
            o_copy(o, d).start()
        at = columns(e * cap, cap)
        recvbuf[d, at, :] = sendbuf[d, at, :]

        @pl.when(d % 2 == 1)
        def _():
            start_pair(gate_pairs + d // 2 + pair_slots)

        @pl.when(jnp.logical_and(d >= lag, d - lag < down_chunks - per_slice))
        def _():
            combine_and_send(d - lag)

        return 0

    lax.fori_loop(0, down_chunks, expert_out, 0)

    def late(d, _):
        combine_and_send(d)
        return 0

    lax.fori_loop(max(0, down_chunks - lag), down_chunks - per_slice, late, 0)
    for c in range(per_slice):
        total = combined(down_chunks - per_slice + c)
        for s in range(1, n_t):
            total += y_arrived(s, c)
        out[:, c * chunk:(c + 1) * chunk] = total.astype(jnp.bfloat16)

    for o in range(1, n_e):
        meta_copy(o).wait_send()
    for s in range(1, n_t):
        z_copy(s).wait_send()

    def drain_blocks(s, _):
        for o in range(n_x):
            if o:
                x_copy(o, s).wait_send()
            d_copy(o, s).wait_send()
        return 0

    lax.fori_loop(0, n_t, drain_blocks, 0)

    def drain_rows(d, _):
        for o in range(1, n_e):
            o_copy(o, d).wait_send()
        return 0

    lax.fori_loop(0, down_chunks, drain_rows, 0)

    def drain_sums(d, _):
        y_copy(d).wait_send()
        return 0

    lax.fori_loop(0, down_chunks - per_slice, drain_sums, 0)


def per_device(n_e, n_t, tokens, norm_gain, w_gate, w_up, w_down, expert_ids, gate_weights):
    rows, width_local = tokens.shape
    width, hid = w_gate.shape
    cap = rows // 2
    slots = n_e * cap
    chunk = min(512, width_local, hid)
    per_slice = width_local // chunk
    down_chunks = n_t * per_slice
    pairs = hid // chunk + down_chunks // 2
    spent = 2 * (width * rows * n_e + slots * width + slots * hid + 2 * slots * width + 2 * rows * width)
    pair_slots = min(pairs, (56 * MIB - spent) // (4 * width * chunk))
    lanes = -(-rows // 128) * 128
    pad = lanes - rows
    meta = jnp.concatenate(
        [
            jnp.pad(expert_ids.T.astype(jnp.float32), ((0, 0), (0, pad)), constant_values=-1.0),
            jnp.pad(gate_weights.T, ((0, 4), (0, pad))),
        ],
        axis=0,
    )
    vmem = pl.BlockSpec(memory_space=pltpu.VMEM)
    hbm = pl.BlockSpec(memory_space=pl.ANY)
    bf16, f32, dma = jnp.bfloat16, jnp.float32, pltpu.SemaphoreType.DMA
    return pl.pallas_call(
        functools.partial(kernel, n_e, n_t, cap, chunk, pair_slots, 3),
        out_shape=jax.ShapeDtypeStruct((rows, width_local), bf16),
        in_specs=[vmem, vmem, vmem, vmem, hbm, hbm, hbm],
        out_specs=vmem,
        scratch_shapes=[
            pltpu.VMEM((2 * pair_slots, width, chunk), bf16),
            pltpu.VMEM((n_e, n_t, rows, width_local), bf16),
            pltpu.VMEM((n_e, 8, lanes), f32),
            pltpu.VMEM((slots, width), bf16),
            pltpu.VMEM((slots, hid), bf16),
            pltpu.VMEM((slots, lanes), f32),
            pltpu.VMEM((rows, slots), bf16),
            pltpu.VMEM((down_chunks, slots, chunk), bf16),
            pltpu.VMEM((down_chunks, slots, chunk), bf16),
            pltpu.VMEM((down_chunks, rows, chunk), bf16),
            pltpu.VMEM((n_t, per_slice, rows, chunk), bf16),
            dma((2 * pair_slots,)),
            dma((2,)),
            dma((n_e, n_t)),
            dma((n_t,)),
            dma((n_e // 2, n_t)),
            dma((n_e // 2, n_t)),
            dma((n_e,)),
            dma((n_e,)),
            dma((n_e, down_chunks)),
            dma((n_e, down_chunks)),
            dma((down_chunks,)),
            dma((n_t, per_slice)),
        ],
        compiler_params=pltpu.CompilerParams(
            collective_id=0, has_side_effects=True, vmem_limit_bytes=67043328
        ),
    )(tokens, norm_gain.reshape(1, width), meta, expert_ids, w_gate, w_up, w_down)


def solution(mesh):
    in_specs = (
        P(("groups", "expert"), "tensor"),
        P(),
        P(None, ("expert", "tensor")),
        P(None, ("expert", "tensor")),
        P(("expert", "tensor"), None),
        P(("groups", "expert"), None),
        P(("groups", "expert"), None),
    )
    out_specs = P(("groups", "expert"), "tensor")
    body = functools.partial(per_device, mesh.shape["expert"], mesh.shape["tensor"])
    return jax.shard_map(body, mesh=mesh, in_specs=in_specs, out_specs=out_specs, check_vma=False)
```

time: 173 us -> 68.2 us (0.39)
  Pallas kernels: 0 us -> 63.1 us
  waiting for transfers between devices: 53 us -> 0 us
  matrix products: 42.3 us -> 0 us
  blocking collectives: 34.6 us -> 0 us
  local copies, waits for them, and re-layouts: 17.2 us -> 2.95 us
  between operations: 13.6 us -> 0.01 us
  other arithmetic: 8.46 us -> 1.95 us
  starting transfers between devices: 3.96 us -> 0 us
    pallas_call x0 -> x1, Pallas kernels: none -> 63.1 us  [per_device(): pl.pallas_call(functools.partial(kernel, n_e, n_t, cap, chunk, pair_slots...]
    dot_general x3 -> x0, matrix products: 42.3 us -> none  [the longest x1 25.3 us: per_device(): partial_value = jnp.dot(hidden, w_down, preferred_element_type=jnp.float32)]
    reduce_scatter x1 -> x0, waiting for transfers between devices: 28.3 us -> none  [per_device(): mixed = lax.psum_scatter(mixed, 'tensor', scatter_dimension=1, tiled=True)]
    all_to_all x1 -> x0, waiting for transfers between devices: 24.7 us -> none  [per_device(): lax.all_to_all(partial_value, 'expert', split_axis=0, concat_axis=0, tile...]
    all_gather x1 -> x0, blocking collectives: 17.6 us -> none  [per_device(): full_rows = lax.all_gather(tokens, 'tensor', axis=1, tiled=True)]
    all_to_all x1 -> x0, blocking collectives: 17 us -> none  [per_device(): lax.all_to_all(outbound, 'expert', split_axis=0, concat_axis=0, tiled=True)]
    gather x3 -> x0, local copies, waits for them, and re-layouts: 9.3 us -> none  [the longest x2 8.11 us: per_device(): picks = jnp.take(by_expert, flat_ids * capacity + slot_of, axis=0)]
    reduce_sum x5 -> x0, other arithmetic: 5.31 us -> none  [the longest x1 4.49 us: per_device(): jnp.sum(picks.reshape(tok_rows, 2, out_width) * gate_weights[:, :, None],...]
  transfers between devices with their start and end apart: 2 -> 0, of which waited for: 2 -> 0; matrix products, arithmetic and copies ran while one was open for 0% -> 0% of each run, Pallas kernels for 0% -> 0%
where the time goes in v1:
time: 68.2 us; the launch traced here: 68 us
  Pallas kernels  63.1 us (93%)
  local copies, waits for them, and re-layouts  2.95 us (4%)
  other arithmetic  1.95 us (3%)
    pallas_call x1, Pallas kernels, per_device(): pl.pallas_call(functools.partial(kernel, n_e, n_t, cap, chunk, pair_slots...  63.1 us
    unnamed x2, local copies, waits for them, and re-layouts  2.95 us

profile of v1, /device:TPU:0, one launch (start us, length us, event | category | flops | bytes accessed | tf_op | source)
XLA Modules:
  0.0 68.0 jit_solution(7246277706427944538)
XLA Ops:
  0.0 0.7 %convert_bitcast_fusion = f32[2,64]{1,0:T(2,128)S(1)} fusion(s32[64,2]{0,1:T(2,128)} %param.12), kind=kLoop, calls=%fused_computation.3 | loop fusion | flops 128 | bytes 1024 | tf_op jit(solution)/shard_map/convert_element_type | solution.py:330
  0.7 1.3 %select_maximum_fusion.meta = f32[8,128]{1,0:T(8,128)} fusion(f32[2,64]{1,0:T(2,128)} %bitcast.5, f32[2,64]{1,0:T(2,128)S(1)} %convert_bitcast_fusion), kind=kLoop, calls=%fused_computation | loop fusion | flops 5120 | bytes 5120 | tf_op jit(solution)/shard_map/concatenate | solution.py:328
  2.0 1.4 %copy.8.ids = s32[64,2]{1,0:T(8,128)} copy(s32[64,2]{0,1:T(2,128)} %param.12) | data formatting | bytes 1024 | tf_op args[5]
  3.3 63.1 %shard_map.73 = bf16[64,1024]{1,0:T(8,128)(2,1)} custom-call(bf16[64,1024]{1,0:T(8,128)(2,1)} %tokens.1, f32[1,4096]{1,0:T(1,128)} %bitcast.4, f32[8,128]{1,0:T(8,128)} %select_maximum_fusion.meta, s32[64,2]{1,0:T(8,128)} %copy.8.ids, bf16[4096,4096]{1,0:T(8,128)(2,1)} %w_gate.1, bf16[4096,4096]{1,0:T(8,128)(2,1)} %w_up.1, bf16[4096,4096]{1,0:T(8,128)(2,1)} %w_down.1), custom_call_target="tpu_custom_call" | custom-call | tf_op jit(solution)/shard_map/pallas_call | solution.py:338
  66.5 1.6 %copy.10 = bf16[64,1024]{1,0:T(8,128)(2,1)} copy(bf16[64,1024]{1,0:T(8,128)(2,1)} %shard_map.73) | data formatting | bytes 262144

commit v2 on v1

--- a/solution.py
+++ b/solution.py
@@ -72,18 +72,29 @@
             send_sem=send_sem, recv_sem=rsem.at[ej, q], device_id=to, device_id_type=MESH,
         )
 
-    def z_copy(s):
-        return block_copy(e, t, zsem.at[s], (g, e, lax.rem(t + s, n_t)))
-
-    def x_copy(o, s):
-        return block_copy(e, lax.rem(t + s, n_t), xsem.at[o, s], (g, lax.rem(xi + o, n_x) * 2 + core, t))
-
-    def d_copy(o, s):
+    def z_copy(side, q):
+        return block_copy(e, q, zsem.at[side, q], (g, e, lax.rem(t + 1 - 2 * side + n_t, n_t)))
+
+    def x_copy(o, q):
+        return block_copy(e, q, xsem.at[o, q], (g, lax.rem(xi + o, n_x) * 2 + core, t))
+
+    def d_copy(o, q):
         ej = lax.rem(xi + o, n_x) * 2 + core
-        return block_copy(ej, lax.rem(t + s, n_t), dsem.at[o, s], (g, sibling, t))
-
-    def arrived(ej, s):
-        block_copy(ej, lax.rem(t + s, n_t), zsem.at[0], (g, sibling, t)).wait_recv()
+        return block_copy(ej, q, dsem.at[o, q], (g, sibling, t))
+
+    def arrived(ej, q):
+        block_copy(ej, q, zsem.at[0, 0], (g, sibling, t)).wait_recv()
+
+    def has_next(side):
+        return t < n_t - 1 if side == 0 else t > 0
+
+    def at_distance(h, step):
+        for side in (0, 1):
+            q = t - h if side == 0 else t + h
+
+            @pl.when(q >= 0 if side == 0 else q < n_t)
+            def _():
+                step(side, q)
 
     def meta_copy(o):
         return pltpu.make_async_remote_copy(
@@ -129,8 +140,10 @@
 
     for o in range(1, n_e):
         meta_copy(o).start()
-    for s in range(1, n_t):
-        z_copy(s).start()
+    for side in (0, 1):
+        @pl.when(has_next(side))
+        def _():
+            z_copy(side, t).start()
 
     lanes = meta.shape[1]
     upper = (
@@ -148,12 +161,12 @@
         return jnp.where(slot == order, 1.0, 0.0) * named
 
     def pack(s):
-        q = lax.rem(t + s, n_t)
+        q = s
 
         def one(ej, _):
             @pl.when(ej % 2 != core)
             def _():
-                arrived(ej, s)
+                arrived(ej, q)
 
             select = pick(ej)[:, :rows].astype(jnp.bfloat16)
             picked = jnp.dot(select, blocks[ej, q], preferred_element_type=jnp.float32)
@@ -172,20 +185,33 @@
             x_copy(o, s).start()
         d_copy(0, s).start()
 
-    forward(0)
+    forward(t)
     for o in range(1, n_e):
         meta_arrived(o)
 
-    def dispatch(s, _):
-        arrived(e, s)
-        forward(s)
-        relay(s - 1)
-        pack(s - 1)
-        return 0
-
-    lax.fori_loop(1, n_t, dispatch, 0)
-    relay(n_t - 1)
-    pack(n_t - 1)
+    def take(side, q):
+        arrived(e, q)
+
+        @pl.when(has_next(side))
+        def _():
+            z_copy(side, q).start()
+
+        forward(q)
+
+    def finish(side, q):
+        relay(q)
+        pack(q)
+
+    at_distance(1, take)
+    finish(0, t)
+
+    def dispatch(h, _):
+        at_distance(h, take)
+        at_distance(h - 1, finish)
+        return 0
+
+    lax.fori_loop(2, n_t, dispatch, 0)
+    at_distance(n_t - 1, finish)
 
     def normalize(ej, _):
         at = columns(ej * cap, cap)
@@ -286,10 +312,13 @@
 
     for o in range(1, n_e):
         meta_copy(o).wait_send()
-    for s in range(1, n_t):
-        z_copy(s).wait_send()
 
     def drain_blocks(s, _):
+        for side in (0, 1):
+            @pl.when(jnp.logical_and(has_next(side), s <= t if side == 0 else s >= t))
+            def _():
+                z_copy(side, s).wait_send()
+
         for o in range(n_x):
             if o:
                 x_copy(o, s).wait_send()
@@ -355,7 +384,7 @@
             dma((2 * pair_slots,)),
             dma((2,)),
             dma((n_e, n_t)),
-            dma((n_t,)),
+            dma((2, n_t)),
             dma((n_e // 2, n_t)),
             dma((n_e // 2, n_t)),
             dma((n_e,)),

time: 68.2 us -> 60.5 us (0.89); the launches traced: 68 us -> 59.6 us
  Pallas kernels: 63.1 us -> 54.7 us
    pallas_call x1, Pallas kernels: 63.1 us -> 54.7 us  [per_device(): pl.pallas_call(functools.partial(kernel, n_e, n_t, cap, chunk, pair_slots...]
where the time goes in v2:
time: 60.5 us; the launch traced here: 59.6 us
  Pallas kernels  54.7 us (90%)
  local copies, waits for them, and re-layouts  2.95 us (5%)
  other arithmetic  1.95 us (3%)
    pallas_call x1, Pallas kernels, per_device(): pl.pallas_call(functools.partial(kernel, n_e, n_t, cap, chunk, pair_slots...  54.7 us
    unnamed x2, local copies, waits for them, and re-layouts  2.95 us
    concatenate x1, other arithmetic, per_device(): jnp.concatenate([jnp.pad(expert_ids.T.astype(jnp.float32), ((0, 0), (0, p...  1.27 us

profile of v2, /device:TPU:0, one launch (start us, length us, event | category | flops | bytes accessed | tf_op | source)
XLA Modules:
  0.0 59.6 jit_solution(11132469241953065448)
XLA Ops:
  0.0 0.7 %convert_bitcast_fusion = f32[2,64]{1,0:T(2,128)S(1)} fusion(s32[64,2]{0,1:T(2,128)} %param.12), kind=kLoop, calls=%fused_computation.3 | loop fusion | flops 128 | bytes 1024 | tf_op jit(solution)/shard_map/convert_element_type | solution.py:359
  0.7 1.3 %select_maximum_fusion.meta = f32[8,128]{1,0:T(8,128)} fusion(f32[2,64]{1,0:T(2,128)} %bitcast.5, f32[2,64]{1,0:T(2,128)S(1)} %convert_bitcast_fusion), kind=kLoop, calls=%fused_computation | loop fusion | flops 5120 | bytes 5120 | tf_op jit(solution)/shard_map/concatenate | solution.py:357
  2.0 1.4 %copy.8.ids = s32[64,2]{1,0:T(8,128)} copy(s32[64,2]{0,1:T(2,128)} %param.12) | data formatting | bytes 1024 | tf_op args[5]
  3.3 54.7 %shard_map.73 = bf16[64,1024]{1,0:T(8,128)(2,1)} custom-call(bf16[64,1024]{1,0:T(8,128)(2,1)} %tokens.1, f32[1,4096]{1,0:T(1,128)} %bitcast.4, f32[8,128]{1,0:T(8,128)} %select_maximum_fusion.meta, s32[64,2]{1,0:T(8,128)} %copy.8.ids, bf16[4096,4096]{1,0:T(8,128)(2,1)} %w_gate.1, bf16[4096,4096]{1,0:T(8,128)(2,1)} %w_up.1, bf16[4096,4096]{1,0:T(8,128)(2,1)} %w_down.1), custom_call_target="tpu_custom_call" | custom-call | tf_op jit(solution)/shard_map/pallas_call | solution.py:367
  58.0 1.6 %copy.10 = bf16[64,1024]{1,0:T(8,128)(2,1)} copy(bf16[64,1024]{1,0:T(8,128)(2,1)} %shard_map.73) | data formatting | bytes 262144
